TPU v7x, 32 devices: a whole 2x2x4 slice. The times are simulated.
32 devices in a mesh: group: 2 (over y), row: 4 (over z), col: 4 (over x, core).
Axes of the slice: x: 2, y: 2, z: 4, core: 2. Of those that a mesh axis runs over, the one named last changes fastest.
Arguments:
- compressed_absorbed_queries: bfloat16 [16, 128, 512], P(('group', 'row')), parts along dimension 0, may hold values from -6 to 6
- query_rope: bfloat16 [16, 64, 128], P(('group', 'row')), parts along dimension 0, may hold values from -6 to 6
- compressed_stored_keys: bfloat16 [16, 1024, 512], P(('group', 'row'), 'col'), parts along dimension 0, may hold values from -32 to 32
- cache_rope: bfloat16 [16, 64, 1024], P(('group', 'row'), None, 'col'), parts along dimension 0, may hold values from -32 to 32
- seq_lengths: int32 [16], P(('group', 'row')), parts along dimension 0, may hold values from 2 to 1024, as said below
- ffn_rows: bfloat16 [64, 7168], P(('group', 'row'), 'col'), parts along dimension 0, may hold values from -6 to 6
- norm_gain: bfloat16 [7168], P('col'), may hold values from 0.099609375 to 1.8984375
- w_gate: bfloat16 [7168, 18432], P('col', 'row'), may hold values from -0.0625 to 0.0625
- w_up: bfloat16 [7168, 18432], P('col', 'row'), may hold values from -0.0625 to 0.0625
- w_down: bfloat16 [18432, 7168], P('row', 'col'), may hold values from -0.046875 to 0.046875
Outputs:
- context: bfloat16 [16, 128, 512], P(('group', 'row'), 'col'), parts along dimension 0
- ffn_out: bfloat16 [64, 7168], P(('group', 'row'), 'col'), parts along dimension 0
There are 2 independent parts, one for each index of `group`. A program takes and returns all parts, laid end to end along the dimension named above; an argument that names none is the same for every part. Nothing has to cross between parts.
Inputs may be any that keep to these rules, and one draw needn't show every extreme that they name: `seq_lengths`: each sequence has 2 to 1024 filled slots, the first ones of its cache, and some sequence has exactly 1024.
All inputs are finite; a program needn't handle non-finite values.
Results may differ from a plain program's by a relative error of at most 0.017.
Values may be sent and summed in bfloat16 or wider, within the bound.
A program may use at most 128 MiB of HBM per device.

v0:
```python
import jax
import jax.numpy as jnp
from jax import lax
from jax.sharding import PartitionSpec as P

NOPE = 128
NEGATIVE_PADDING = -1e30


def joined(x, axis, combine):
    everything = jax.tree.map(
        lambda part, kind: lax.all_gather(part.astype(kind), axis),
        x,
        (jnp.bfloat16, jnp.bfloat16, jnp.bfloat16),
    )

    def take(k):
        return jax.tree.map(lambda part, own: part[k].astype(own.dtype), everything, x)

    return lax.fori_loop(
        1, lax.axis_size(axis), lambda k, so_far: combine(so_far, take(k)), take(0)
    )


def local_partials(
    compressed_absorbed_queries,
    query_rope,
    compressed_stored_keys,
    cache_rope,
    seq_lengths,
    first_pos,
):
    similarity_logits = jnp.einsum(
        "zxm,zum->zxu",
        compressed_absorbed_queries,
        compressed_stored_keys,
        preferred_element_type=jnp.float32,
    )
    similarity_logits = similarity_logits + jnp.einsum(
        "srh,srl->shl", query_rope, cache_rope, preferred_element_type=jnp.float32
    )
    similarity_logits = similarity_logits * (NOPE + query_rope.shape[1]) ** (-0.5)
    position = first_pos + jnp.arange(compressed_stored_keys.shape[1], dtype=jnp.int32)
    visible = position[None, None, :] < seq_lengths[:, None, None]
    similarity_logits = jnp.where(visible, similarity_logits, NEGATIVE_PADDING)
    top_score = jnp.max(similarity_logits, axis=2)
    weights = jnp.where(visible, jnp.exp(similarity_logits - top_score[:, :, None]), 0.0)
    denominator = jnp.sum(weights, axis=2)
    weighted = jnp.einsum(
        "jac,jcw->jaw",
        weights.astype(jnp.bfloat16),
        compressed_stored_keys,
        preferred_element_type=jnp.float32,
    )
    return (top_score, denominator, weighted)


def join_partials(earlier, later):
    top_score = jnp.maximum(earlier[0], later[0])
    left_factor = jnp.exp(earlier[0] - top_score)
    right_factor = jnp.exp(later[0] - top_score)
    denominator = earlier[1] * left_factor + later[1] * right_factor
    weighted = earlier[2] * left_factor[:, :, None] + later[2] * right_factor[:, :, None]
    return (top_score, denominator, weighted)


def on_device(
    compressed_absorbed_queries,
    query_rope,
    compressed_stored_keys,
    cache_rope,
    seq_lengths,
    ffn_rows,
    norm_gain,
    w_gate,
    w_up,
    w_down,
):
    column_position = lax.axis_index("col")
    first_pos = column_position * compressed_stored_keys.shape[1]
    top_score, denominator, weighted = local_partials(
        compressed_absorbed_queries,
        query_rope,
        compressed_stored_keys,
        cache_rope,
        seq_lengths,
        first_pos,
    )
    head_share = compressed_absorbed_queries.shape[1] // lax.axis_size("col")
    merged = joined((top_score, denominator, weighted), "col", join_partials)
    own_total = lax.dynamic_slice_in_dim(merged[1], column_position * head_share, head_share, 1)
    own_weighted = lax.dynamic_slice_in_dim(merged[2], column_position * head_share, head_share, 1)
    context = (own_weighted / own_total[:, :, None]).astype(jnp.bfloat16)
    rows_wide = ffn_rows.astype(jnp.float32)
    square_sums = lax.psum(jnp.sum(rows_wide * rows_wide, axis=1), "col")
    full_width = ffn_rows.shape[1] * lax.axis_size("col")
    reciprocal_norm = lax.rsqrt(square_sums / full_width + 1e-06)
    normed = (rows_wide * reciprocal_norm[:, None] * norm_gain.astype(jnp.float32)[None, :]).astype(
        jnp.bfloat16
    )
    shard_rows = lax.all_gather(normed, "row", axis=0, tiled=True)
    gate_part = jnp.dot(shard_rows, w_gate, preferred_element_type=jnp.float32)
    up_part = jnp.dot(shard_rows, w_up, preferred_element_type=jnp.float32)
    projected = jnp.concatenate([gate_part, up_part], axis=1)
    units = w_gate.shape[1]
    share_sums = lax.psum_scatter(
        projected.astype(jnp.bfloat16), "col", scatter_dimension=0, tiled=True
    ).astype(jnp.float32)
    hidden_share = (jax.nn.silu(share_sums[:, :units]) * share_sums[:, units:]).astype(jnp.bfloat16)
    hidden = lax.all_gather(hidden_share, "col", axis=0, tiled=True)
    reduced_total = lax.psum_scatter(
        jnp.dot(hidden, w_down, preferred_element_type=jnp.float32),
        "row",
        scatter_dimension=0,
        tiled=True,
    )
    ffn_out = (rows_wide + reduced_total).astype(jnp.bfloat16)
    return (context, ffn_out)


def solution(mesh):
    return jax.shard_map(
        on_device,
        mesh=mesh,
        in_specs=(
            P(("group", "row"), None, None),
            P(("group", "row"), None, None),
            P(("group", "row"), "col", None),
            P(("group", "row"), None, "col"),
            P(("group", "row")),
            P(("group", "row"), "col"),
            P("col"),
            P("col", "row"),
            P("col", "row"),
            P("row", "col"),
        ),
        out_specs=(P(("group", "row"), "col", None), P(("group", "row"), "col")),
        check_vma=False,
    )
```

profile of v0, /device:TPU:0, one launch (start us, length us, event | category | flops | bytes accessed | tf_op | source)
XLA Modules:
  0.0 115.1 jit_solution(4013423057301016343)
XLA Ops:
  7.2 0.9 fusion.14
  8.2 0.7 convert_element_type.125
  8.8 8.3 %psum.7 = f32[8]{0:T(128)S(1)} all-reduce(f32[8]{0:T(128)S(1)} %fusion.14), channel_id=1, replica_groups=mesh['group'=2,'row'=4,'col'=4] {'col'}, use_global_device_ids=true, to_apply=%region_5.6 | all-reduce | flops 8 | bytes 64 | tf_op jit(solution)/shard_map/psum | solution.py:95
  17.2 1.0 fusion.16
  18.2 13.7 %all_gather.24 = bf16[32,1792]{1,0:T(8,128)(2,1)S(1)} all-gather(bf16[8,1792]{1,0:T(8,128)(2,1)S(1)} %fusion.16), channel_id=1, replica_groups=mesh['group'=2,'row'=4,'col'=4] {'row'}, dimensions={0}, use_global_device_ids=true | all-gather | bytes 143360 | tf_op jit(solution)/shard_map/all_gather | solution.py:101
  31.9 8.6 %convolution_convert_fusion = bf16[32,4608]{1,0:T(8,128)(2,1)S(1)} fusion(bf16[32,1792]{1,0:T(8,128)(2,1)S(1)} %all_gather.24, bf16[1792,4608]{1,0:T(8,128)(2,1)} %param.20), kind=kOutput, calls=%fused_computation.12 | convolution fusion | flops 528629760 | bytes 16924672 | tf_op jit(solution)/shard_map/dot_general | solution.py:103
  40.6 2.9 %convolution_convert_fusion.1 = bf16[32,4608]{1,0:T(8,128)(2,1)S(1)} fusion(bf16[32,1792]{1,0:T(8,128)(2,1)S(1)} %all_gather.24, bf16[1792,4608]{1,0:T(8,128)(2,1)S(1)} %copy-done.1), kind=kOutput, calls=%fused_computation.13 | convolution fusion | flops 528629760 | bytes 16924672 | tf_op jit(solution)/shard_map/dot_general | solution.py:102
  43.5 0.9 pad_maximum_fusion
  44.4 0.0 all-gather.7.cloned.1.call-start
  44.5 0.1 broadcast_compare_fusion
  44.5 0.2 fusion.23
  44.8 0.4 fusion.22
  45.2 1.0 convolution_convert_fusion.2
  46.2 0.0 reduce-scatter.5.cloned.1.call-start
  46.2 0.2 fusion.8
  46.4 5.1 %all-gather.4 = bf16[4,2,128]{2,1,0:T(2,128)(2,1)S(1)} all-gather(bf16[1,2,128]{2,1,0:T(2,128)(2,1)S(1)} %bitcast.49), channel_id=3, replica_groups=mesh['group'=2,'row'=4,'col'=4] {'col'}, dimensions={0}, use_global_device_ids=true | all-gather | bytes 2560 | tf_op jit(solution)/shard_map/all_gather | solution.py:12
  51.5 5.0 %all-gather.3 = bf16[4,2,128]{2,1,0:T(2,128)(2,1)S(1)} all-gather(bf16[1,2,128]{2,1,0:T(2,128)(2,1)S(1)} %convert_bitcast_fusion.1), channel_id=2, replica_groups=mesh['group'=2,'row'=4,'col'=4] {'col'}, dimensions={0}, use_global_device_ids=true | all-gather | bytes 2560 | tf_op jit(solution)/shard_map/all_gather | solution.py:12
  56.6 10.2 %reduce-scatter.3.cloned.1.call-done = bf16[8,9216]{1,0:T(8,128)(2,1)} async-done(((bf16[32,9216]{1,0:T(8,128)(2,1)}), bf16[8,9216]{1,0:T(8,128)(2,1)}) %reduce-scatter.3.cloned.1.call-update) | async-done | bytes 147472 | tf_op jit(solution)/shard_map/reduce_scatter | solution.py:106
  66.8 0.9 convert_element_type.127
  67.7 0.1 fusion.9
  67.8 5.9 %all_gather.25 = bf16[32,4608]{1,0:T(8,128)(2,1)S(1)} all-gather(bf16[8,4608]{1,0:T(8,128)(2,1)S(1)} %fusion.9), channel_id=1, replica_groups=mesh['group'=2,'row'=4,'col'=4] {'col'}, dimensions={0}, use_global_device_ids=true | all-gather | bytes 368640 | tf_op jit(solution)/shard_map/all_gather | solution.py:110
  73.6 9.6 %fusion.24 = f32[32,1792]{1,0:T(8,128)} fusion(bf16[32,4608]{1,0:T(8,128)(2,1)S(1)} %all_gather.25, bf16[4608,1792]{1,0:T(8,128)(2,1)} %param.21), kind=kOutput, calls=%fused_computation.49 | convolution fusion | flops 528482304 | bytes 17039360 | tf_op jit(solution)/shard_map/dot_general | solution.py:112
  83.3 1.8 %all-gather.7.cloned.1.call-done = bf16[8,128,512]{2,1,0:T(8,128)(2,1)} async-done(((bf16[2,128,512]{2,1,0:T(8,128)(2,1)}), bf16[8,128,512]{2,1,0:T(8,128)(2,1)}) %all-gather.7.cloned.1.call-update) | async-done | bytes 1048592 | tf_op jit(solution)/shard_map/all_gather | solution.py:12
  85.1 1.0 slice_convert_fusion
  86.1 3.5 %while.19 = (s32[]{:T(128)}, f32[2,128]{1,0:T(2,128)S(1)}, f32[2,128]{1,0:T(2,128)S(1)}, f32[2,128,512]{2,1,0:T(8,128)S(1)}, bf16[4,2,128]{2,1,0:T(2,128)(2,1)S(...) while((s32[]{:T(128)}, f32[2,128]{1,0:T(2,128)S(1)}, ...), condition=%wide.region_3.4_spmd, body=%wide.region_2.3_spmd.sunk | while | flops 526341 | bytes 1320087 | solution.py:20
  86.1 1.1 fusion.39
  87.3 1.1 fusion.39
  88.5 1.1 fusion.39
  89.6 0.1 constant_dynamic-slice_fusion.2
  89.7 0.7 divide_convert_fusion
  90.4 16.8 %reduce-scatter.5.cloned.1.call-done = f32[8,1792]{1,0:T(8,128)} async-done(((f32[32,1792]{1,0:T(8,128)}), f32[8,1792]{1,0:T(8,128)}) %reduce-scatter.5.cloned.1.call-update) | async-done | bytes 57360 | tf_op jit(solution)/shard_map/reduce_scatter | solution.py:111
  107.2 1.4 %fusion.17 = bf16[8,1792]{1,0:T(8,128)(2,1)} fusion(f32[8,1792]{1,0:T(8,128)} %reduce-scatter.5.cloned.1.call-done, bf16[8,1792]{1,0:T(8,128)(2,1)S(1)} %copy-done.3), kind=kLoop, calls=%fused_computation.35 | loop fusion | flops 43008 | bytes 114688 | tf_op jit(solution)/shard_map/convert_element_type | solution.py:117
  (26 shorter events, 0.2 us)
Async XLA Ops:
  7.2 37.6 %copy-start = (bf16[2,256,512]{2,1,0:T(8,128)(2,1)S(1)}, bf16[2,256,512]{2,1,0:T(8,128)(2,1)}, u32[]{:S(2)}) copy-start(bf16[2,256,512]{2,1,0:T(8,128)(2,1)} %param.14) | copy-start | bytes 1572868
  7.2 59.6 %reduce-scatter.3.cloned.1.call-start = ((), (), s32[]{:S(2)}) async-start(), calls=%async_computation.2 | async-start | bytes 737280 | tf_op jit(solution)/shard_map/reduce_scatter | solution.py:106
  17.2 23.3 %copy-start.1 = (bf16[1792,4608]{1,0:T(8,128)(2,1)S(1)}, bf16[1792,4608]{1,0:T(8,128)(2,1)}, u32[]{:S(2)}) copy-start(bf16[1792,4608]{1,0:T(8,128)(2,1)} %param.19) | copy-start | bytes 49545220
  40.5 3.9 %copy-start.6 = (s32[2]{0:T(128)S(1)}, s32[2]{0:T(128)}, u32[]{:S(2)}) copy-start(s32[2]{0:T(128)} %param.16) | copy-start | bytes 28
  40.5 4.0 %copy-start.4 = (bf16[2,64,256]{2,1,0:T(8,128)(2,1)S(1)}, bf16[2,64,256]{2,1,0:T(8,128)(2,1)}, u32[]{:S(2)}) copy-start(bf16[2,64,256]{2,1,0:T(8,128)(2,1)} %param.15) | copy-start | bytes 196612
  40.5 4.0 %copy-start.5 = (bf16[2,64,128]{2,1,0:T(8,128)(2,1)S(1)}, bf16[2,64,128]{2,1,0:T(8,128)(2,1)}, u32[]{:S(2)}) copy-start(bf16[2,64,128]{2,1,0:T(8,128)(2,1)} %param.13) | copy-start | bytes 98308
  40.6 4.2 %copy-start.2 = (bf16[2,128,512]{2,1,0:T(8,128)(2,1)S(1)}, bf16[2,128,512]{2,1,0:T(8,128)(2,1)}, u32[]{:S(2)}) copy-start(bf16[2,128,512]{2,1,0:T(8,128)(2,1)} %param.12) | copy-start | bytes 786436
  44.4 40.7 %all-gather.7.cloned.1.call-start = ((), (), s32[]{:S(2)}) async-start(), calls=%async_computation.4 | async-start | bytes 1310720 | tf_op jit(solution)/shard_map/all_gather | solution.py:12
  46.2 61.0 %reduce-scatter.5.cloned.1.call-start = ((), (), s32[]{:S(2)}) async-start(), calls=%async_computation.3 | async-start | bytes 286720 | tf_op jit(solution)/shard_map/reduce_scatter | solution.py:111
  67.8 39.4 %copy-start.3 = (bf16[8,1792]{1,0:T(8,128)(2,1)S(1)}, bf16[8,1792]{1,0:T(8,128)(2,1)}, u32[]{:S(2)}) copy-start(bf16[8,1792]{1,0:T(8,128)(2,1)} %param.17) | copy-start | bytes 86020
Sparse Core Ops, SparseCore 0:
  44.5 22.2 reduce-scatter.2
  68.3 16.6 all-gather.6
  87.3 19.8 reduce-scatter.4
where the time goes:
time: 116 us; the launch traced here: 115 us
  blocking collectives  38.1 us (33%)
  waiting for transfers between devices  28.8 us (25%)
  matrix products  22.7 us (20%)
  between operations  13.9 us (12%)
  other arithmetic  11.3 us (10%)
    reduce_scatter x1, waiting for transfers between devices, on_device(): lax.psum_scatter(jnp.dot(hidden, w_down, preferred_element_type=jnp.float...  16.8 us
    all_gather x1, blocking collectives, on_device(): shard_rows = lax.all_gather(normed, 'row', axis=0, tiled=True)  13.7 us
    reduce_scatter x1, waiting for transfers between devices, on_device(): lax.psum_scatter(projected.astype(jnp.bfloat16), 'col', scatter_dimension...  10.2 us
    all_gather x2, blocking collectives, joined(): lax.all_gather(part.astype(kind), axis)  10.1 us
    dot_general x1, matrix products, on_device(): jnp.dot(hidden, w_down, preferred_element_type=jnp.float32)  9.63 us
    dot_general x1, matrix products, on_device(): up_part = jnp.dot(shard_rows, w_up, preferred_element_type=jnp.float32)  8.62 us
    psum x1, blocking collectives, on_device(): square_sums = lax.psum(jnp.sum(rows_wide * rows_wide, axis=1), 'col')  8.34 us
    all_gather x1, blocking collectives, on_device(): hidden = lax.all_gather(hidden_share, 'col', axis=0, tiled=True)  5.87 us
  transfers between devices with their start and end apart: 3, of which 3 were waited for; matrix products, arithmetic and copies ran while one was open for 15% of the time, Pallas kernels for 0%

commit v1 on v0

--- a/solution.py
+++ b/solution.py
@@ -92,7 +92,7 @@
     own_weighted = lax.dynamic_slice_in_dim(merged[2], column_position * head_share, head_share, 1)
     context = (own_weighted / own_total[:, :, None]).astype(jnp.bfloat16)
     rows_wide = ffn_rows.astype(jnp.float32)
-    square_sums = lax.psum(jnp.sum(rows_wide * rows_wide, axis=1), "col")
+    square_sums = jnp.sum(lax.all_gather(jnp.sum(rows_wide * rows_wide, axis=1), "col"), axis=0)
     full_width = ffn_rows.shape[1] * lax.axis_size("col")
     reciprocal_norm = lax.rsqrt(square_sums / full_width + 1e-06)
     normed = (rows_wide * reciprocal_norm[:, None] * norm_gain.astype(jnp.float32)[None, :]).astype(

time: 116 us -> 118 us (1.017)
  local copies, waits for them, and re-layouts: 0.12 us -> 1.69 us
    unnamed x0 -> x1, blocking collectives: none -> 8.34 us
    psum x1 -> x0, blocking collectives: 8.34 us -> none  [on_device(): square_sums = lax.psum(jnp.sum(rows_wide * rows_wide, axis=1), 'col')]
    unnamed x14 -> x17, local copies, waits for them, and re-layouts: 0.04 us -> 1.53 us
where the time goes in v1:
time: 118 us
  blocking collectives  38.1 us (32%)
  waiting for transfers between devices  28.8 us (24%)
  matrix products  22.8 us (19%)
  between operations  14.6 us (12%)
  other arithmetic  11.5 us (10%)
  local copies, waits for them, and re-layouts  1.69 us (1%)
    reduce_scatter x1, waiting for transfers between devices, on_device(): lax.psum_scatter(jnp.dot(hidden, w_down, preferred_element_type=jnp.float...  16.8 us
    all_gather x1, blocking collectives, on_device(): shard_rows = lax.all_gather(normed, 'row', axis=0, tiled=True)  13.7 us
    reduce_scatter x1, waiting for transfers between devices, on_device(): lax.psum_scatter(projected.astype(jnp.bfloat16), 'col', scatter_dimension...  10.2 us
    all_gather x2, blocking collectives, joined(): lax.all_gather(part.astype(kind), axis)  10.1 us
    dot_general x1, matrix products, on_device(): jnp.dot(hidden, w_down, preferred_element_type=jnp.float32)  9.62 us
    dot_general x1, matrix products, on_device(): up_part = jnp.dot(shard_rows, w_up, preferred_element_type=jnp.float32)  8.62 us
    unnamed x1, blocking collectives  8.34 us
    all_gather x1, blocking collectives, on_device(): hidden = lax.all_gather(hidden_share, 'col', axis=0, tiled=True)  5.87 us
  transfers between devices with their start and end apart: 3, of which 3 were waited for; matrix products, arithmetic and copies ran while one was open for 15% of the time, Pallas kernels for 0%

profile of v1, /device:TPU:0, one launch (start us, length us, event | category | flops | bytes accessed | tf_op | source)
XLA Modules:
  0.0 117.5 jit_solution(16787793843505300926)
XLA Ops:
  7.2 0.9 fusion.14
  8.2 1.2 %dynamic-slice = u32[1]{0:T(128)} dynamic-slice(u32[32]{0:T(128)} %constant.71, u32[]{:T(128)S(6)} %add.97), dynamic_slice_sizes={1} | dynamic-slice | bytes 12
  10.1 0.2 dynamic-update-slice
  10.3 8.3 %all-reduce = f32[32]{0:T(128)S(1)} all-reduce(f32[32]{0:T(128)S(1)} %dynamic-update-slice), channel_id=5, replica_groups=mesh['group'=2,'row'=4,'col'=4] {'col'}, use_global_device_ids=true, to_apply=%add | all-reduce | flops 32 | bytes 256
  18.6 0.1 reshape.84
  18.8 0.8 convert_element_type.125
  19.6 1.0 fusion.16
  20.6 13.7 %all_gather.32 = bf16[32,1792]{1,0:T(8,128)(2,1)S(1)} all-gather(bf16[8,1792]{1,0:T(8,128)(2,1)S(1)} %fusion.16), channel_id=1, replica_groups=mesh['group'=2,'row'=4,'col'=4] {'row'}, dimensions={0}, use_global_device_ids=true | all-gather | bytes 143360 | tf_op jit(solution)/shard_map/all_gather | solution.py:101
  34.3 8.6 %convolution_convert_fusion = bf16[32,4608]{1,0:T(8,128)(2,1)S(1)} fusion(bf16[32,1792]{1,0:T(8,128)(2,1)S(1)} %all_gather.32, bf16[1792,4608]{1,0:T(8,128)(2,1)} %param.20), kind=kOutput, calls=%fused_computation.12 | convolution fusion | flops 528629760 | bytes 16924672 | tf_op jit(solution)/shard_map/dot_general | solution.py:103
  43.0 2.9 %convolution_convert_fusion.1 = bf16[32,4608]{1,0:T(8,128)(2,1)S(1)} fusion(bf16[32,1792]{1,0:T(8,128)(2,1)S(1)} %all_gather.32, bf16[1792,4608]{1,0:T(8,128)(2,1)S(1)} %copy-done.1), kind=kOutput, calls=%fused_computation.13 | convolution fusion | flops 528629760 | bytes 16924672 | tf_op jit(solution)/shard_map/dot_general | solution.py:102
  45.9 0.9 pad_maximum_fusion
  46.9 0.1 broadcast_compare_fusion
  46.9 0.2 fusion.23
  47.2 0.4 fusion.22
  47.6 1.0 convolution_convert_fusion.2
  48.7 0.2 fusion.8
  48.9 5.1 %all-gather.5 = bf16[4,2,128]{2,1,0:T(2,128)(2,1)S(1)} all-gather(bf16[1,2,128]{2,1,0:T(2,128)(2,1)S(1)} %bitcast.50), channel_id=3, replica_groups=mesh['group'=2,'row'=4,'col'=4] {'col'}, dimensions={0}, use_global_device_ids=true | all-gather | bytes 2560 | tf_op jit(solution)/shard_map/all_gather | solution.py:12
  53.9 5.0 %all-gather.4 = bf16[4,2,128]{2,1,0:T(2,128)(2,1)S(1)} all-gather(bf16[1,2,128]{2,1,0:T(2,128)(2,1)S(1)} %convert_bitcast_fusion.1), channel_id=2, replica_groups=mesh['group'=2,'row'=4,'col'=4] {'col'}, dimensions={0}, use_global_device_ids=true | all-gather | bytes 2560 | tf_op jit(solution)/shard_map/all_gather | solution.py:12
  59.0 10.2 %reduce-scatter.3.cloned.1.call-done = bf16[8,9216]{1,0:T(8,128)(2,1)} async-done(((bf16[32,9216]{1,0:T(8,128)(2,1)}), bf16[8,9216]{1,0:T(8,128)(2,1)}) %reduce-scatter.3.cloned.1.call-update) | async-done | bytes 147472 | tf_op jit(solution)/shard_map/reduce_scatter | solution.py:106
  69.2 0.9 convert_element_type.127
  70.2 5.9 %all_gather.33 = bf16[32,4608]{1,0:T(8,128)(2,1)S(1)} all-gather(bf16[8,4608]{1,0:T(8,128)(2,1)S(1)} %fusion.9), channel_id=1, replica_groups=mesh['group'=2,'row'=4,'col'=4] {'col'}, dimensions={0}, use_global_device_ids=true | all-gather | bytes 368640 | tf_op jit(solution)/shard_map/all_gather | solution.py:110
  76.0 9.6 %fusion.24 = f32[32,1792]{1,0:T(8,128)} fusion(bf16[32,4608]{1,0:T(8,128)(2,1)S(1)} %all_gather.33, bf16[4608,1792]{1,0:T(8,128)(2,1)} %param.21), kind=kOutput, calls=%fused_computation.49 | convolution fusion | flops 528482304 | bytes 17039360 | tf_op jit(solution)/shard_map/dot_general | solution.py:112
  85.7 1.8 %all-gather.8.cloned.1.call-done = bf16[8,128,512]{2,1,0:T(8,128)(2,1)} async-done(((bf16[2,128,512]{2,1,0:T(8,128)(2,1)}), bf16[8,128,512]{2,1,0:T(8,128)(2,1)}) %all-gather.8.cloned.1.call-update) | async-done | bytes 1048592 | tf_op jit(solution)/shard_map/all_gather | solution.py:12
  87.5 1.0 slice_convert_fusion
  88.5 3.5 %while.19 = (s32[]{:T(128)}, f32[2,128]{1,0:T(2,128)S(1)}, f32[2,128]{1,0:T(2,128)S(1)}, f32[2,128,512]{2,1,0:T(8,128)S(1)}, bf16[4,2,128]{2,1,0:T(2,128)(2,1)S(...) while((s32[]{:T(128)}, f32[2,128]{1,0:T(2,128)S(1)}, ...), condition=%wide.region_3.4_spmd, body=%wide.region_2.3_spmd.sunk | while | flops 526341 | bytes 1320087 | solution.py:20
  88.5 1.1 fusion.39
  89.7 1.1 fusion.39
  90.9 1.1 fusion.39
  92.0 0.1 constant_dynamic-slice_fusion.2
  92.1 0.7 divide_convert_fusion
  92.8 16.8 %reduce-scatter.5.cloned.1.call-done = f32[8,1792]{1,0:T(8,128)} async-done(((f32[32,1792]{1,0:T(8,128)}), f32[8,1792]{1,0:T(8,128)}) %reduce-scatter.5.cloned.1.call-update) | async-done | bytes 57360 | tf_op jit(solution)/shard_map/reduce_scatter | solution.py:111
  109.6 1.4 %fusion.17 = bf16[8,1792]{1,0:T(8,128)(2,1)} fusion(f32[8,1792]{1,0:T(8,128)} %reduce-scatter.5.cloned.1.call-done, bf16[8,1792]{1,0:T(8,128)(2,1)S(1)} %copy-done.3), kind=kLoop, calls=%fused_computation.35 | loop fusion | flops 43008 | bytes 114688 | tf_op jit(solution)/shard_map/convert_element_type | solution.py:117
  (31 shorter events, 0.4 us)
Async XLA Ops:
  7.2 40.0 %copy-start = (bf16[2,256,512]{2,1,0:T(8,128)(2,1)S(1)}, bf16[2,256,512]{2,1,0:T(8,128)(2,1)}, u32[]{:S(2)}) copy-start(bf16[2,256,512]{2,1,0:T(8,128)(2,1)} %param.14) | copy-start | bytes 1572868
  7.2 62.0 %reduce-scatter.3.cloned.1.call-start = ((), (), s32[]{:S(2)}) async-start(), calls=%async_computation.2 | async-start | bytes 737280 | tf_op jit(solution)/shard_map/reduce_scatter | solution.py:106
  18.7 24.2 %copy-start.1 = (bf16[1792,4608]{1,0:T(8,128)(2,1)S(1)}, bf16[1792,4608]{1,0:T(8,128)(2,1)}, u32[]{:S(2)}) copy-start(bf16[1792,4608]{1,0:T(8,128)(2,1)} %param.19) | copy-start | bytes 49545220
  42.9 3.9 %copy-start.6 = (s32[2]{0:T(128)S(1)}, s32[2]{0:T(128)}, u32[]{:S(2)}) copy-start(s32[2]{0:T(128)} %param.16) | copy-start | bytes 28
  42.9 4.0 %copy-start.4 = (bf16[2,64,256]{2,1,0:T(8,128)(2,1)S(1)}, bf16[2,64,256]{2,1,0:T(8,128)(2,1)}, u32[]{:S(2)}) copy-start(bf16[2,64,256]{2,1,0:T(8,128)(2,1)} %param.15) | copy-start | bytes 196612
  42.9 4.0 %copy-start.5 = (bf16[2,64,128]{2,1,0:T(8,128)(2,1)S(1)}, bf16[2,64,128]{2,1,0:T(8,128)(2,1)}, u32[]{:S(2)}) copy-start(bf16[2,64,128]{2,1,0:T(8,128)(2,1)} %param.13) | copy-start | bytes 98308
  43.0 4.2 %copy-start.2 = (bf16[2,128,512]{2,1,0:T(8,128)(2,1)S(1)}, bf16[2,128,512]{2,1,0:T(8,128)(2,1)}, u32[]{:S(2)}) copy-start(bf16[2,128,512]{2,1,0:T(8,128)(2,1)} %param.12) | copy-start | bytes 786436
  46.8 40.7 %all-gather.8.cloned.1.call-start = ((), (), s32[]{:S(2)}) async-start(), calls=%async_computation.4 | async-start | bytes 1310720 | tf_op jit(solution)/shard_map/all_gather | solution.py:12
  48.6 61.0 %reduce-scatter.5.cloned.1.call-start = ((), (), s32[]{:S(2)}) async-start(), calls=%async_computation.3 | async-start | bytes 286720 | tf_op jit(solution)/shard_map/reduce_scatter | solution.py:111
  70.2 39.4 %copy-start.3 = (bf16[8,1792]{1,0:T(8,128)(2,1)S(1)}, bf16[8,1792]{1,0:T(8,128)(2,1)}, u32[]{:S(2)}) copy-start(bf16[8,1792]{1,0:T(8,128)(2,1)} %param.17) | copy-start | bytes 86020
Sparse Core Ops, SparseCore 0:
  46.9 22.2 reduce-scatter.2
  70.7 16.6 all-gather.7
  89.7 19.8 reduce-scatter.4
